TPU v7x, 128 devices: a whole 4x4x4 slice. The times are simulated.
128 devices in a mesh: dp: 8 (over z_hi, y), mp: 8 (over z_lo, x), outer: 2 (over core).
Axes of the slice: x: 4, y: 4, z: 4 (z_hi: 2, z_lo: 2; z = z_hi * 2 + z_lo), core: 2. Of those that a mesh axis runs over, the one named last changes fastest.
Arguments:
- activations: bfloat16 [32768, 8192], P(('dp', 'outer'), 'mp'), may hold values from -6 to 6
- act_scale: float32 [256, 64], P(('dp', 'outer'), 'mp'), may hold values from 0.25 to 4
- out_grads: bfloat16 [32768, 16384], P(('dp', 'outer'), 'mp'), may hold values from -6 to 6
- gradient_tile_scale: float32 [256, 128], P(('dp', 'outer'), 'mp'), may hold values from 0.25 to 4
- prior_input_factor: float32 [8, 1024, 1024], P('mp', ('dp', 'outer')), may hold values from -0.3 to 6, as said below
- g_factor: float32 [16, 1024, 1024], P('mp', ('dp', 'outer')), may hold values from -0.3 to 6, as said below
- weight_grad: bfloat16 [8192, 16384], P('mp', ('dp', 'outer')), may hold values from -6 to 6
- a_inverse: bfloat16 [8, 1024, 1024], P('mp', ('dp', 'outer')), as said below
- g_inverse: bfloat16 [16, 1024, 1024], P(('dp', 'outer'), 'mp'), as said below
Outputs:
- a_stat: float32 [8, 1024, 1024], P('mp', ('dp', 'outer'))
- g_stat: float32 [16, 1024, 1024], P('mp', ('dp', 'outer'))
- new_a_factor: float32 [8, 1024, 1024], P('mp', ('dp', 'outer'))
- new_g_factor: float32 [16, 1024, 1024], P('mp', ('dp', 'outer'))
- preconditioned: bfloat16 [8192, 16384], P('mp', ('dp', 'outer'))
Inputs may be any that keep to these rules, and one draw needn't show every extreme that they name: `a_inverse`: each block is the identity plus dense off-diagonal and diagonal entries of magnitude at most 1.5 / sqrt(1024). `g_inverse`: each block is the identity plus dense off-diagonal and diagonal entries of magnitude at most 1.5 / sqrt(1024). `prior_input_factor`: each block is symmetric with a positive diagonal. `g_factor`: each block is symmetric with a positive diagonal.
All inputs are finite; a program needn't handle non-finite values.
Results may differ from a plain program's by a relative error of at most 0.014.
Values may be sent and summed in bfloat16 or wider, within the bound.
A program may use at most 128 MiB of HBM per device.

v0:
```python
import jax
import jax.numpy as jnp
from jax import lax
from jax.sharding import PartitionSpec as P

BLK = 1024
QT = 128
EMA_DECAY = 0.95


def dequantize(quantized, tile_scale):
    row_total, column_total = quantized.shape
    tiles_with_scale = (
        quantized.reshape(row_total // QT, QT, column_total // QT, QT)
        * tile_scale[:, None, :, None]
    )
    return tiles_with_scale.reshape(row_total, column_total).astype(jnp.bfloat16)


def body(
    activations,
    act_scale,
    out_grads,
    gradient_tile_scale,
    prior_input_factor,
    g_factor,
    weight_grad,
    a_inverse,
    g_inverse,
):
    input_factor_tiles = dequantize(activations, act_scale).reshape(activations.shape[0], -1, BLK)
    gradient_factor_tiles = dequantize(out_grads, gradient_tile_scale).reshape(
        out_grads.shape[0], -1, BLK
    )
    input_count = input_factor_tiles.shape[1]
    activation_rows = jnp.einsum(
        "qym,qyx->myx", input_factor_tiles, input_factor_tiles, preferred_element_type=jnp.float32
    )
    gradient_rows = jnp.einsum(
        "qym,qyx->myx",
        gradient_factor_tiles,
        gradient_factor_tiles,
        preferred_element_type=jnp.float32,
    )
    summed = lax.psum_scatter(
        jnp.concatenate([activation_rows, gradient_rows], axis=1).astype(jnp.bfloat16),
        ("dp", "outer"),
        scatter_dimension=0,
        tiled=True,
    ).astype(jnp.float32)
    token_total = activations.shape[0] * lax.axis_size("dp") * lax.axis_size("outer")
    statistics = jnp.transpose(summed, (1, 0, 2)) / token_total
    a_stat = statistics[:input_count]
    g_stat = statistics[input_count:]
    new_a_factor = EMA_DECAY * prior_input_factor + (1.0 - EMA_DECAY) * a_stat
    new_g_factor = EMA_DECAY * g_factor + (1.0 - EMA_DECAY) * g_stat
    row_blocks = weight_grad.shape[0] // BLK
    column_blocks = weight_grad.shape[1] // BLK
    grad_blocks = weight_grad.reshape(row_blocks, BLK, column_blocks, BLK)
    right = jnp.einsum(
        "aigk,gkl->aigl",
        grad_blocks,
        lax.all_gather(g_inverse, "mp", axis=1, tiled=True),
        preferred_element_type=jnp.float32,
    ).astype(jnp.bfloat16)
    result = jnp.einsum(
        "aij,ajgl->aigl",
        lax.all_gather(a_inverse, ("dp", "outer"), axis=1, tiled=True),
        right,
        preferred_element_type=jnp.float32,
    ).astype(jnp.bfloat16)
    return (
        a_stat,
        g_stat,
        new_a_factor,
        new_g_factor,
        result.reshape(row_blocks * BLK, column_blocks * BLK),
    )


def solution(mesh):
    return jax.shard_map(
        body,
        mesh=mesh,
        in_specs=(
            P(("dp", "outer"), "mp"),
            P(("dp", "outer"), "mp"),
            P(("dp", "outer"), "mp"),
            P(("dp", "outer"), "mp"),
            P("mp", ("dp", "outer"), None),
            P("mp", ("dp", "outer"), None),
            P("mp", ("dp", "outer")),
            P("mp", ("dp", "outer"), None),
            P(("dp", "outer"), "mp", None),
        ),
        out_specs=(
            P("mp", ("dp", "outer"), None),
            P("mp", ("dp", "outer"), None),
            P("mp", ("dp", "outer"), None),
            P("mp", ("dp", "outer"), None),
            P("mp", ("dp", "outer")),
        ),
        check_vma=False,
    )
```

profile of v0, /device:TPU:0, one launch (start us, length us, event | category | flops | bytes accessed | tf_op | source)
XLA Modules:
  0.0 278.4 jit_solution(16005743546915442506)
XLA Ops:
  7.2 0.0 all-gather.3.cloned.1.call-start
  7.2 0.7 all-gather.3.cloned.1.call-update
  7.9 0.0 all-gather.5.cloned.1.call-start
  8.0 0.7 all-gather.5.cloned.1.call-update
  8.7 0.0 all-reduce.3.cloned.1.call-start
  8.7 0.8 copy.36
  9.5 0.6 mul.46
  10.1 9.6 %convert_bitcast_fusion.2 = bf16[1024,1,1024]{0,2,1:T(8,128)(2,1)S(1)} fusion(f32[256,8,8,128]{3,2,1,0:T(8,128)S(1)} %bitcast.55, bf16[2048,1024]{1,0:T(8,128)(2,1)} %param.9), kind=kOutput, calls=%fused_computation.17 | convolution fusion | flops 4302307328 | bytes 14680064 | tf_op jit(solution)/shard_map/qym,qyx->myx/dot_general | solution.py:36
  19.7 1.1 mul.49
  20.8 11.8 %fusion = bf16[2048,2048]{1,0:T(8,128)(2,1)} fusion(f32[256,8,16,128]{3,2,1,0:T(8,128)S(1)} %bitcast.54, bf16[2048,2048]{1,0:T(8,128)(2,1)} %param.11), kind=kLoop, calls=%fused_computation.1 | loop fusion | flops 12582912 | bytes 33554432 | tf_op jit(solution)/shard_map/convert_element_type | solution.py:17
  32.6 13.8 %convert_bitcast_fusion = bf16[1024,2,1024]{0,2,1:T(8,128)(2,1)S(1)} fusion(bf16[256,2,8,1024]{3,2,1,0:T(8,128)(2,1)} %bitcast.56), kind=kOutput, calls=%fused_computation.9 | convolution fusion | flops 8592031744 | bytes 12582912 | tf_op jit(solution)/shard_map/qym,qyx->myx/dot_general | solution.py:39
  46.4 3.2 %pad_maximum_fusion = bf16[1024,3,1024]{0,2,1:T(8,128)(2,1)} fusion(bf16[1024,2,1024]{0,2,1:T(8,128)(2,1)S(1)} %convert_bitcast_fusion, bf16[1024,1,1024]{0,2,1:T(8,128)(2,1)S(1)} %convert_bitcast_fusion.2), kind=kLoop, calls=%fused_computation.7 | loop fusion | flops 3145728 | bytes 12582912 | tf_op jit(solution)/shard_map/concatenate | solution.py:46
  49.6 14.4 %copy.39 = bf16[1024,3,1024]{2,1,0:T(4,128)(2,1)} copy(bf16[1024,3,1024]{0,2,1:T(8,128)(2,1)} %pad_maximum_fusion) | data formatting | bytes 12582912 | tf_op jit(solution)/shard_map/concatenate | solution.py:46
  64.0 0.6 copy-done.4
  64.7 0.6 dynamic-slice
  65.9 0.0 all-gather.3.cloned.1.call-done
  65.9 37.5 %all-gather.5.cloned.1.call-done = bf16[1,1024,1024]{2,1,0:T(8,128)(2,1)} async-done(((bf16[1,64,1024]{2,1,0:T(8,128)(2,1)}), bf16[1,1024,1024]{2,1,0:T(8,128)(2,1)}) %all-gather.5.cloned.1.call-update) | async-done | bytes 2097168 | tf_op jit(solution)/shard_map/all_gather | solution.py:68
  103.5 8.1 %convert_bitcast_fusion.1 = bf16[1024,1024]{0,1:T(8,128)(2,1)} fusion(bf16[1,1024,1024]{2,1,0:T(8,128)(2,1)} %all-gather.5.cloned.1.call-done, bf16[1024,1024]{1,0:T(8,128)(2,1)S(1)} %copy-done, bf16[1,1024,1024]{2,1,0:T(8,128)(2,1)} %all-gather.3.cloned.1.call-done), kind=kOutput, calls=%fused_computation.15 | convolution fusion | flops 4297064448 | bytes 8388608 | tf_op jit(solution)/shard_map/aij,ajgl->aigl/dot_general | solution.py:66
  111.6 4.0 %copy.41 = bf16[1024,1024]{1,0:T(8,128)(2,1)} copy(bf16[1024,1024]{0,1:T(8,128)(2,1)} %convert_bitcast_fusion.1) | data formatting | bytes 4194304
  115.6 152.9 %all-reduce.3.cloned.1.call-done = bf16[1024,3,1024]{2,1,0:T(4,128)(2,1)} async-done(((bf16[1024,3,1024]{2,1,0:T(4,128)(2,1)}), bf16[1024,3,1024]{2,1,0:T(4,128)(2,1)}) %all-reduce.3.cloned.1.call-update) | async-done | bytes 6291472
  268.5 1.2 constant_dynamic-slice_fusion
  269.7 0.2 multiply_bitcast_fusion
  269.9 1.1 multiply_add_fusion
  271.0 0.8 multiply_add_fusion.1
  (10 shorter events, 0.0 us)
Async XLA Ops:
  7.2 96.3 %copy-start = (bf16[1024,1024]{1,0:T(8,128)(2,1)S(1)}, bf16[1024,1024]{1,0:T(8,128)(2,1)}, u32[]{:S(2)}) copy-start(bf16[1024,1024]{1,0:T(8,128)(2,1)} %param.15) | copy-start | bytes 6291460
  7.2 58.7 %all-gather.3.cloned.1.call-start = ((), (), s32[]{:S(2)}) async-start(), calls=%async_computation | async-start | bytes 2359296 | tf_op jit(solution)/shard_map/all_gather | solution.py:63
  7.9 95.6 %all-gather.5.cloned.1.call-start = ((), (), s32[]{:S(2)}) async-start(), calls=%async_computation.1 | async-start | bytes 2228224 | tf_op jit(solution)/shard_map/all_gather | solution.py:68
  8.7 259.8 %all-reduce.3.cloned.1.call-start = ((), (), s32[]{:S(2)}) async-start(), calls=%async_computation.2 | async-start | bytes 16777216
  10.1 9.6 %copy-start.3 = (f32[16,16]{1,0:T(8,128)S(1)}, f32[16,16]{1,0:T(8,128)}, u32[]{:S(2)}) copy-start(f32[16,16]{1,0:T(8,128)} %param.12) | copy-start | bytes 3076
  64.0 0.7 copy-start.4
  111.6 158.4 %copy-start.1 = (f32[2,64,1024]{2,1,0:T(8,128)S(1)}, f32[2,64,1024]{2,1,0:T(8,128)}, u32[]{:S(2)}) copy-start(f32[2,64,1024]{2,1,0:T(8,128)} %param.14) | copy-start | bytes 1572868
  111.6 159.5 %copy-start.2 = (f32[1,64,1024]{2,1,0:T(8,128)S(1)}, f32[1,64,1024]{2,1,0:T(8,128)}, u32[]{:S(2)}) copy-start(f32[1,64,1024]{2,1,0:T(8,128)} %param.13) | copy-start | bytes 786436
Sparse Core Ops, SparseCore 0:
  9.6 43.7 all-gather.2
  55.8 47.5 all-gather.4
  106.0 162.4 all-reduce.2
where the time goes:
time: 279 us; the launch traced here: 278 us
  waiting for transfers between devices  192 us (69%)
  matrix products  31.4 us (11%)
  local copies, waits for them, and re-layouts  23.4 us (8%)
  other arithmetic  17.1 us (6%)
  between operations  14.5 us (5%)
    unnamed x4, waiting for transfers between devices  154 us
    all_gather x1, waiting for transfers between devices, body(): lax.all_gather(a_inverse, ('dp', 'outer'), axis=1, tiled=True)  37.5 us
    concatenate x1, local copies, waits for them, and re-layouts, body(): jnp.concatenate([activation_rows, gradient_rows], axis=1)  14.4 us
    dot_general x1, matrix products, body(): jnp.einsum('qym,qyx->myx', gradient_factor_tiles, gradient_factor_tiles,...  13.8 us
    convert_element_type x1, other arithmetic, dequantize(): tiles_with_scale.reshape(row_total, column_total).astype(jnp.bfloat16)  11.8 us
    dot_general x1, matrix products, body(): jnp.einsum('qym,qyx->myx', input_factor_tiles, input_factor_tiles, prefer...  9.56 us
    dot_general x1, matrix products, body(): jnp.einsum('aij,ajgl->aigl', lax.all_gather(a_inverse, ('dp', 'outer'), a...  8.1 us
    unnamed x14, local copies, waits for them, and re-layouts  7.24 us
  transfers between devices with their start and end apart: 3, of which 2 were waited for; matrix products, arithmetic and copies ran while one was open for 24% of the time, Pallas kernels for 0%

commit v1 on v0

--- a/solution.py
+++ b/solution.py
@@ -65,7 +65,12 @@
     ).astype(jnp.bfloat16)
     result = jnp.einsum(
         "aij,ajgl->aigl",
-        lax.all_gather(a_inverse, ("dp", "outer"), axis=1, tiled=True),
+        jnp.concatenate(
+            lax.all_to_all(
+                jnp.stack([a_inverse] * lax.axis_size(("dp", "outer"))), ("dp", "outer"), 0, 0
+            ),
+            axis=1,
+        ),
         right,
         preferred_element_type=jnp.float32,
     ).astype(jnp.bfloat16)

time: 279 us -> 264 us (0.946)
  waiting for transfers between devices: 192 us -> 165 us
  starting transfers between devices: 0.11 us -> 8.14 us
    all_gather x1 -> x0, waiting for transfers between devices: 37.5 us -> none  [body(): lax.all_gather(a_inverse, ('dp', 'outer'), axis=1, tiled=True)]
    all_to_all x0 -> x1, waiting for transfers between devices: none -> 36.3 us  [body(): lax.all_to_all(jnp.stack([a_inverse] * lax.axis_size(('dp', 'outer'))), (...]
    unnamed x4 -> x3, waiting for transfers between devices: 154 us -> 129 us
    all_to_all x0 -> x1, starting transfers between devices: none -> 8.06 us  [body(): lax.all_to_all(jnp.stack([a_inverse] * lax.axis_size(('dp', 'outer'))), (...]
    unnamed x14 -> x16, local copies, waits for them, and re-layouts: 7.24 us -> 7.48 us
  transfers between devices with their start and end apart: 3 -> 3, of which waited for: 2 -> 2; matrix products, arithmetic and copies ran while one was open for 24% -> 26% of each run, Pallas kernels for 0% -> 0%
where the time goes in v1:
time: 264 us
  waiting for transfers between devices  165 us (62%)
  matrix products  31.5 us (12%)
  local copies, waits for them, and re-layouts  25.2 us (10%)
  other arithmetic  17.2 us (7%)
  between operations  16.2 us (6%)
  starting transfers between devices  8.14 us (3%)
    unnamed x3, waiting for transfers between devices  129 us
    all_to_all x1, waiting for transfers between devices, body(): lax.all_to_all(jnp.stack([a_inverse] * lax.axis_size(('dp', 'outer'))), (...  36.3 us
    concatenate x1, local copies, waits for them, and re-layouts, body(): jnp.concatenate([activation_rows, gradient_rows], axis=1)  14.4 us
    dot_general x1, matrix products, body(): jnp.einsum('qym,qyx->myx', gradient_factor_tiles, gradient_factor_tiles,...  13.8 us
    convert_element_type x1, other arithmetic, dequantize(): tiles_with_scale.reshape(row_total, column_total).astype(jnp.bfloat16)  11.8 us
    dot_general x1, matrix products, body(): jnp.einsum('qym,qyx->myx', input_factor_tiles, input_factor_tiles, prefer...  9.56 us
    dot_general x1, matrix products, body(): jnp.einsum('aij,ajgl->aigl', jnp.concatenate(lax.all_to_all(jnp.stack([a_...  8.19 us
    all_to_all x1, starting transfers between devices, body(): lax.all_to_all(jnp.stack([a_inverse] * lax.axis_size(('dp', 'outer'))), (...  8.06 us
  transfers between devices with their start and end apart: 3, of which 2 were waited for; matrix products, arithmetic and copies ran while one was open for 26% of the time, Pallas kernels for 0%

profile of v1, /device:TPU:0, one launch (start us, length us, event | category | flops | bytes accessed | tf_op | source)
XLA Modules:
  0.0 263.7 jit_solution(4347682718428510238)
XLA Ops:
  8.0 0.0 all-gather.2.cloned.1.call-start
  8.1 0.7 all-gather.2.cloned.1.call-update
  8.7 0.0 all-reduce.3.cloned.1.call-start
  8.8 0.8 copy.36
  9.6 0.6 mul.46
  10.2 9.6 %convert_bitcast_fusion.2 = bf16[1024,1,1024]{0,2,1:T(8,128)(2,1)S(1)} fusion(f32[256,8,8,128]{3,2,1,0:T(8,128)S(1)} %bitcast.53, bf16[2048,1024]{1,0:T(8,128)(2,1)} %param.9), kind=kOutput, calls=%fused_computation.16 | convolution fusion | flops 4302307328 | bytes 14680064 | tf_op jit(solution)/shard_map/qym,qyx->myx/dot_general | solution.py:36
  19.8 1.1 mul.49
  20.9 11.8 %fusion = bf16[2048,2048]{1,0:T(8,128)(2,1)} fusion(f32[256,8,16,128]{3,2,1,0:T(8,128)S(1)} %bitcast.52, bf16[2048,2048]{1,0:T(8,128)(2,1)} %param.11), kind=kLoop, calls=%fused_computation.1 | loop fusion | flops 12582912 | bytes 33554432 | tf_op jit(solution)/shard_map/convert_element_type | solution.py:17
  32.7 13.8 %convert_bitcast_fusion = bf16[1024,2,1024]{0,2,1:T(8,128)(2,1)S(1)} fusion(bf16[256,2,8,1024]{3,2,1,0:T(8,128)(2,1)} %bitcast.54), kind=kOutput, calls=%fused_computation.9 | convolution fusion | flops 8592031744 | bytes 12582912 | tf_op jit(solution)/shard_map/qym,qyx->myx/dot_general | solution.py:39
  46.5 3.2 %pad_maximum_fusion = bf16[1024,3,1024]{0,2,1:T(8,128)(2,1)} fusion(bf16[1024,2,1024]{0,2,1:T(8,128)(2,1)S(1)} %convert_bitcast_fusion, bf16[1024,1,1024]{0,2,1:T(8,128)(2,1)S(1)} %convert_bitcast_fusion.2), kind=kLoop, calls=%fused_computation.7 | loop fusion | flops 3145728 | bytes 12582912 | tf_op jit(solution)/shard_map/concatenate | solution.py:46
  49.7 14.4 %copy.39 = bf16[1024,3,1024]{2,1,0:T(4,128)(2,1)} copy(bf16[1024,3,1024]{0,2,1:T(8,128)(2,1)} %pad_maximum_fusion) | data formatting | bytes 12582912 | tf_op jit(solution)/shard_map/concatenate | solution.py:46
  64.1 0.0 all-reduce.3.cloned.1.call-update
  64.2 0.9 copy-done.3
  65.0 1.6 stack.2
  66.6 8.1 %all-to-all-start = ((bf16[16,1,64,1024]{3,2,1,0:T(8,128)(2,1)}), bf16[16,1,64,1024]{3,2,1,0:T(8,128)(2,1)}, u32[]{:S(2)}, u32[]{:S(2)}) async-start(bf16[16,1,64,1024]{3,2,1,0:T(8,128)(2,1)} %stack.2), calls=%async_computation | async-start | bytes 4194304 | tf_op jit(solution)/shard_map/all_to_all | solution.py:69
  74.7 0.6 dynamic-slice
  75.9 36.3 %all-to-all-done = bf16[16,1,64,1024]{3,2,1,0:T(8,128)(2,1)} async-done(((bf16[16,1,64,1024]{3,2,1,0:T(8,128)(2,1)}), bf16[16,1,64,1024]{3,2,1,0:T(8,128)(2,1)}, u32[]{:S(2)}, u32[]{:S(2)}) %all-to-all-start) | async-done | bytes 2097184 | tf_op jit(solution)/shard_map/all_to_all | solution.py:69
  112.2 8.2 %convert_bitcast_fusion.1 = bf16[1024,1024]{0,1:T(8,128)(2,1)} fusion(bf16[1024,1024]{1,0:T(8,128)(2,1)} %bitcast.9, bf16[1024,1024]{1,0:T(8,128)(2,1)S(1)} %copy-done, bf16[1,1024,1024]{2,1,0:T(8,128)(2,1)} %all-gather.2.cloned.1.call-done), kind=kOutput, calls=%fused_computation.14 | convolution fusion | flops 4297064448 | bytes 8388608 | tf_op jit(solution)/shard_map/aij,ajgl->aigl/dot_general | solution.py:66
  120.4 4.0 %copy.41 = bf16[1024,1024]{1,0:T(8,128)(2,1)} copy(bf16[1024,1024]{0,1:T(8,128)(2,1)} %convert_bitcast_fusion.1) | data formatting | bytes 4194304
  124.4 128.5 %all-reduce.3.cloned.1.call-done = bf16[1024,3,1024]{2,1,0:T(4,128)(2,1)} async-done(((bf16[1024,3,1024]{2,1,0:T(4,128)(2,1)}), bf16[1024,3,1024]{2,1,0:T(4,128)(2,1)}) %all-reduce.3.cloned.1.call-update) | async-done | bytes 6291472
  252.9 1.2 constant_dynamic-slice_fusion
  254.1 0.2 multiply_bitcast_fusion
  254.3 1.1 multiply_add_fusion
  255.4 0.8 multiply_add_fusion.1
  (12 shorter events, 0.0 us)
Async XLA Ops:
  8.0 104.2 %copy-start = (bf16[1024,1024]{1,0:T(8,128)(2,1)S(1)}, bf16[1024,1024]{1,0:T(8,128)(2,1)}, u32[]{:S(2)}) copy-start(bf16[1024,1024]{1,0:T(8,128)(2,1)} %param.15) | copy-start | bytes 6291460
  8.0 104.2 %all-gather.2.cloned.1.call-start = ((), (), s32[]{:S(2)}) async-start(), calls=%async_computation.1 | async-start | bytes 2359296 | tf_op jit(solution)/shard_map/all_gather | solution.py:63
  8.7 244.1 %all-reduce.3.cloned.1.call-start = ((), (), s32[]{:S(2)}) async-start(), calls=%async_computation.2 | async-start | bytes 16777216
  10.2 9.6 %copy-start.4 = (f32[16,16]{1,0:T(8,128)S(1)}, f32[16,16]{1,0:T(8,128)}, u32[]{:S(2)}) copy-start(f32[16,16]{1,0:T(8,128)} %param.12) | copy-start | bytes 3076
  64.1 0.9 copy-start.3
  64.1 10.5 %copy-start.5 = (u32[128]{0:T(128)S(1)}, u32[128]{0:T(128)}, u32[]{:S(2)}) copy-start(u32[128]{0:T(128)} %constant.15) | copy-start | bytes 1540
  66.6 45.6 %all-to-all-start = ((bf16[16,1,64,1024]{3,2,1,0:T(8,128)(2,1)}), bf16[16,1,64,1024]{3,2,1,0:T(8,128)(2,1)}, u32[]{:S(2)}, u32[]{:S(2)}) async-start(bf16[16,1,64,1024]{3,2,1,0:T(8,128)(2,1)} %stack.2), calls=%async_computation | async-start | bytes 4194304 | tf_op jit(solution)/shard_map/all_to_all | solution.py:69
  120.4 133.9 %copy-start.1 = (f32[2,64,1024]{2,1,0:T(8,128)S(1)}, f32[2,64,1024]{2,1,0:T(8,128)}, u32[]{:S(2)}) copy-start(f32[2,64,1024]{2,1,0:T(8,128)} %param.14) | copy-start | bytes 1572868
  120.4 135.0 %copy-start.2 = (f32[1,64,1024]{2,1,0:T(8,128)S(1)}, f32[1,64,1024]{2,1,0:T(8,128)}, u32[]{:S(2)}) copy-start(f32[1,64,1024]{2,1,0:T(8,128)} %param.13) | copy-start | bytes 786436
Sparse Core Ops, SparseCore 0:
  10.5 43.7 all-gather.1
Sparse Core Ops, SparseCore 1:
  64.2 188.6 all-reduce.2
